TPU v7x, 32 devices: a whole 2x2x4 slice. The times are simulated.
32 devices in a mesh: row: 16 (over z, y, core), col: 2 (over x).
Axes of the slice: x: 2, y: 2, z: 4, core: 2. Of those that a mesh axis runs over, the one named last changes fastest.
Arguments:
- positions: float32 [3, 8192], P(None, ('row', 'col')), as said below
- velocities: float32 [3, 8192], P(None, ('row', 'col')), may hold values from -6 to 6
- old_forces: float32 [3, 8192], P(None, ('row', 'col')), may hold values from -6 to 6
- charges: float32 [8192], P(('row', 'col')), may hold values from -3 to 3
- atom_types: int32 [8192], P(('row', 'col')), may hold values from 0 to 7
- type_table: float32 [7, 8], replicated, may hold values from 0.003 to 2, as said below
- tile_pairs: int32 [16, 2, 2, 32], P('row', 'col'), may hold values from -1 to 31, as said below
Outputs:
- new_positions: float32 [3, 8192], P(None, ('row', 'col'))
- new_velocities: float32 [3, 8192], P(None, ('row', 'col'))
- new_forces: float32 [3, 8192], P(None, ('row', 'col'))
Inputs may be any that keep to these rules, and one draw needn't show every extreme that they name: `positions`: the atoms of one block lie together in a cube of its own; the blocks' cubes fill a cubic lattice in the order of the block numbers, at about 0.1 atoms per cubic angstrom. `tile_pairs`: on each device the first n slots hold distinct pairs (a, g) with a below 4 and g below 32, each a tile whose blocks' cubes lie within 12 angstrom of each other; the other slots hold -1 in both entries. n is at most 32, differs from device to device, and equals 32 on the device with the most such tiles when it has 32 or more; the list is a sampled part of each device's near tiles, not all of them. `type_table`: Rows: intrinsic radii 1 to 2, screening scales 0.15 to 0.6, neck weights 0.003 to 0.012, alpha 0.6 to 1, beta 0.3 to 0.9, gamma 0.2 to 0.6, masses 0.5 to 2.
All inputs are finite; a program needn't handle non-finite values.
Results may differ from a plain program's by a relative error of at most 0.0003.
Values sent between devices are 32-bit elements; how exact they have to be, the bound alone decides.
A program may use at most 64 MiB of HBM per device.

v0:
```python
import jax
import jax.numpy as jnp
from jax import lax
from jax.sharding import PartitionSpec as P

TILE = 128
BLK_DEV = 2
GROUP = 4
CUTOFF = 12.0
COULOMB = 32.0
TIMESTEP = 0.5
OFFSET = 0.09
NECK_GAP = 0.5
NECK_WIDTH = 16.0


def taper(dist_sq):
    taper_base = jnp.maximum(1.0 - dist_sq / (CUTOFF * CUTOFF), 0.0)
    return (taper_base * taper_base, -2.0 * taper_base / (CUTOFF * CUTOFF))


def screening(dist_sq, intrinsic, other_radius, other_scale, other_neck):
    soft_sq = dist_sq + intrinsic * intrinsic
    neck_gap = intrinsic + other_radius + NECK_GAP
    neck_off = dist_sq - neck_gap * neck_gap
    neck_bump = jnp.exp(-neck_off * neck_off / NECK_WIDTH)
    volume = other_scale * other_radius * other_radius * other_radius
    descreen = volume / (soft_sq * soft_sq) + other_neck * neck_bump
    slope = -2.0 * volume / (soft_sq * soft_sq * soft_sq) - other_neck * neck_bump * neck_off * (
        2.0 / NECK_WIDTH
    )
    weight, w_slope = taper(dist_sq)
    return (weight * descreen, w_slope * descreen + weight * slope)


def separation(coords_i, coords_j):
    offset_vec = coords_i[:, :, :, None] - coords_j[:, :, None, :]
    return (offset_vec, jnp.sum(offset_vec * offset_vec, axis=1))


def born_terms(side_i, side_j, mask):
    offset_vec, dist_sq = separation(side_i[:, 0:3], side_j[:, 0:3])
    value, slope = screening(
        dist_sq,
        side_i[:, 4][:, :, None],
        side_j[:, 4][:, None, :],
        side_j[:, 5][:, None, :],
        side_j[:, 6][:, None, :],
    )
    return jnp.sum(mask * value, axis=2)[:, None, :]


def pair_terms(side_i, side_j, mask):
    offset_vec, dist_sq = separation(side_i[:, 0:3], side_j[:, 0:3])
    charge_pair = side_i[:, 3][:, :, None] * side_j[:, 3][:, None, :]
    radius_j = side_j[:, -1][:, None, :]
    radii_prod = side_i[:, -1][:, :, None] * radius_j
    radii_exp = jnp.exp(-dist_sq / (4.0 * radii_prod))
    inv_eff = 1.0 / jnp.sqrt(dist_sq + radii_prod * radii_exp)
    inv_cube = inv_eff * inv_eff * inv_eff
    weight, w_slope = taper(dist_sq)
    d_dist = (
        mask
        * charge_pair
        * (w_slope * inv_eff - 0.5 * weight * (1.0 - 0.25 * radii_exp) * inv_cube)
    )
    d_radius = (
        mask
        * -0.5
        * weight
        * charge_pair
        * inv_cube
        * radii_exp
        * (1.0 + dist_sq / (4.0 * radii_prod))
        * radius_j
    )
    direct = 2.0 * COULOMB * jnp.sum(d_dist[:, None] * offset_vec, axis=3)
    return jnp.concatenate([direct, jnp.sum(d_radius, axis=2)[:, None, :]], axis=1)


def chain_terms(side_i, side_j, mask):
    offset_vec, dist_sq = separation(side_i[:, 0:3], side_j[:, 0:3])
    value_ij, slope_ij = screening(
        dist_sq,
        side_i[:, 4][:, :, None],
        side_j[:, 4][:, None, :],
        side_j[:, 5][:, None, :],
        side_j[:, 6][:, None, :],
    )
    value_ji, slope_ji = screening(
        dist_sq,
        side_j[:, 4][:, None, :],
        side_i[:, 4][:, :, None],
        side_i[:, 5][:, :, None],
        side_i[:, 6][:, :, None],
    )
    factor = mask * (side_i[:, -1][:, :, None] * slope_ij + side_j[:, -1][:, None, :] * slope_ji)
    return -2.0 * jnp.sum(factor[:, None] * offset_vec, axis=3)


def radius_terms(born_sum, intrinsic, coef_alpha, coef_beta, coef_gamma):
    scaled = intrinsic * born_sum
    poly_arg = (
        coef_alpha * scaled - coef_beta * scaled * scaled + coef_gamma * scaled * scaled * scaled
    )
    squash = jnp.tanh(poly_arg)
    radius = 1.0 / (1.0 / intrinsic - squash / (intrinsic + OFFSET))
    poly_slope = coef_alpha - 2.0 * coef_beta * scaled + 3.0 * coef_gamma * scaled * scaled
    radius_rate = (
        radius * radius * (1.0 - squash * squash) * poly_slope * intrinsic / (intrinsic + OFFSET)
    )
    return (radius, radius_rate)


def run_tiles(func, rows, pack_i, pack_j, tiles_i, tiles_j, live_f, self_pair, group_count):
    block_total = pack_i.shape[1]
    diagonal = jnp.eye(TILE, dtype=jnp.float32)
    block_ids = jnp.arange(block_total, dtype=jnp.int32)

    def one_turn(turn_index, summed):
        first = turn_index * GROUP
        group_i = lax.dynamic_slice_in_dim(tiles_i, first, GROUP)
        group_j = lax.dynamic_slice_in_dim(tiles_j, first, GROUP)
        group_live = lax.dynamic_slice_in_dim(live_f, first, GROUP)
        group_self = lax.dynamic_slice_in_dim(self_pair, first, GROUP)
        side_i = jnp.moveaxis(jnp.take(pack_i, group_i, axis=1), 1, 0)
        side_j = jnp.moveaxis(jnp.take(pack_j, group_j, axis=1), 1, 0)
        mask = group_live[:, None, None] * (1.0 - group_self[:, None, None] * diagonal)
        partial_sums = func(side_i, side_j, mask)
        owner = (group_i[:, None] == block_ids[None, :]).astype(jnp.float32)
        return summed + jnp.einsum(
            "gk,gra->kra", owner, partial_sums, precision=lax.Precision.HIGHEST
        )

    summed = lax.fori_loop(
        0, group_count, one_turn, jnp.zeros((block_total, rows, TILE), jnp.float32)
    )
    return jnp.moveaxis(summed, 1, 0).reshape(rows, block_total * TILE)


def body(positions, velocities, old_forces, charges, atom_types, type_table, tile_pairs):
    col_count = lax.axis_size("col")
    row_count = lax.axis_size("row")
    col_index = lax.axis_index("col")
    row_index = lax.axis_index("row")
    own_count = positions.shape[1]
    type_ids = jnp.arange(type_table.shape[1], dtype=jnp.int32)
    onehot = (atom_types[None, :] == type_ids[:, None]).astype(jnp.float32)
    params = jnp.sum(type_table[:, :, None] * onehot[None, :, :], axis=1)
    atom_mass = params[6]
    new_positions = (
        positions + TIMESTEP * velocities + TIMESTEP * TIMESTEP / (2.0 * atom_mass) * old_forces
    )
    own_data = jnp.concatenate([new_positions, charges[None, :], params[0:6]], axis=0)
    side_i = lax.all_gather(own_data, "col", axis=1, tiled=True)
    side_j = lax.all_gather(own_data[0:7], "row", axis=1, tiled=True)
    blocks_i = col_count * BLK_DEV
    blocks_j = row_count * BLK_DEV
    pack_i = side_i.reshape(10, blocks_i, TILE)
    pack_j = side_j.reshape(7, blocks_j, TILE)
    tile_list = tile_pairs[0, 0]
    live_slot = tile_list[0] >= 0
    tiles_i = jnp.maximum(tile_list[0], 0)
    tiles_j = jnp.maximum(tile_list[1], 0)
    global_i = row_index * blocks_i + tiles_i
    global_j = (tiles_j // BLK_DEV * col_count + col_index) * BLK_DEV + tiles_j % BLK_DEV
    self_pair = (global_i == global_j).astype(jnp.float32)
    live_f = live_slot.astype(jnp.float32)
    group_count = (jnp.sum(live_slot.astype(jnp.int32)) + GROUP - 1) // GROUP

    def tile_sweep(func, rows, data_i, data_j):
        return run_tiles(
            func, rows, data_i, data_j, tiles_i, tiles_j, live_f, self_pair, group_count
        )

    born_part = tile_sweep(born_terms, 1, pack_i, pack_j)[0]
    born_all = lax.psum(born_part, "col")
    radius_i, rate_i = radius_terms(born_all, side_i[4], side_i[7], side_i[8], side_i[9])
    radius_own = lax.dynamic_slice_in_dim(radius_i, col_index * own_count, own_count)
    radius_j = lax.all_gather(radius_own, "row", axis=0, tiled=True)
    with_radius_i = jnp.concatenate([pack_i, radius_i.reshape(1, blocks_i, TILE)], axis=0)
    with_radius_j = jnp.concatenate([pack_j, radius_j.reshape(1, blocks_j, TILE)], axis=0)
    pair_part = tile_sweep(pair_terms, 4, with_radius_i, with_radius_j)
    grad_all = lax.psum(pair_part[3], "col")
    chain_i = (
        COULOMB * side_i[3] * side_i[3] / (2.0 * radius_i * radius_i) - COULOMB * grad_all
    ) * rate_i
    chain_own = lax.dynamic_slice_in_dim(chain_i, col_index * own_count, own_count)
    chain_j = lax.all_gather(chain_own, "row", axis=0, tiled=True)
    with_chain_i = jnp.concatenate([pack_i, chain_i.reshape(1, blocks_i, TILE)], axis=0)
    with_chain_j = jnp.concatenate([pack_j, chain_j.reshape(1, blocks_j, TILE)], axis=0)
    chain_part = tile_sweep(chain_terms, 3, with_chain_i, with_chain_j)
    force_sum = pair_part[0:3] + chain_part
    new_forces = lax.psum_scatter(force_sum, "col", scatter_dimension=1, tiled=True)
    new_velocities = velocities + TIMESTEP / (2.0 * atom_mass) * (old_forces + new_forces)
    return (new_positions, new_velocities, new_forces)


def solution(mesh):
    return jax.shard_map(
        body,
        mesh=mesh,
        in_specs=(
            P(None, ("row", "col")),
            P(None, ("row", "col")),
            P(None, ("row", "col")),
            P(("row", "col")),
            P(("row", "col")),
            P(),
            P("row", "col", None, None),
        ),
        out_specs=(P(None, ("row", "col")), P(None, ("row", "col")), P(None, ("row", "col"))),
        check_vma=False,
    )
```

profile of v0, /device:TPU:0, one launch (start us, length us, event | category | flops | bytes accessed | tf_op | source)
XLA Modules:
  0.0 163.2 jit_solution(18386366832432704033)
XLA Ops:
  7.2 1.4 maximum_bitcast_fusion
  9.3 0.7 copy-done.8
  9.9 0.7 copy-done.5
  10.8 0.6 copy-done.2
  11.4 0.7 copy-done.9
  12.1 5.3 %all_gather.12 = f32[10,512]{1,0:T(8,128)S(1)} all-gather(f32[10,256]{1,0:T(8,128)S(1)} %pad_maximum_fusion.4), channel_id=1, replica_groups=mesh['row'=16,'col'=2] {'col'}, dimensions={1}, use_global_device_ids=true | all-gather | bytes 30720 | tf_op jit(solution)/shard_map/all_gather | solution.py:155
  17.5 0.7 copy-done.7
  18.2 0.7 slice-done
  18.9 22.5 %all_gather.13 = f32[7,4096]{1,0:T(8,128)S(1)} all-gather(f32[7,256]{1,0:T(8,128)S(1)} %slice-done), channel_id=1, replica_groups=mesh['row'=16,'col'=2] {'row'}, dimensions={1}, use_global_device_ids=true | all-gather | bytes 121856 | tf_op jit(solution)/shard_map/all_gather | solution.py:156
  41.5 2.5 %while.37 = (s32[]{:T(128)}, f32[4,1,128]{2,0,1:T(4,128)S(1)}, s32[]{:T(128)}, s32[32]{0:T(128)S(1)}, f32[32]{0:T(128)S(1)}, /*index=5*/f32[32]{0:T(128)S(1)}, f...) while((s32[]{:T(128)}, f32[4,1,128]{2,0,1:T(4,128)S(1)}, ...), condition=%wide.region_5.6_spmd.clone, body=%wide.region_2.5_spmd.clone.sunk | while | flops 2036306 | bytes 881111 | solution.py:135
  41.6 0.6 gather_fusion.1
  42.2 0.6 gather_fusion
  43.4 0.4 fusion.112
  44.0 11.9 %psum.14 = f32[512]{0:T(512)S(1)} all-reduce(f32[512]{0:T(512)S(1)} %bitcast.173), channel_id=1, replica_groups=mesh['row'=16,'col'=2] {'col'}, use_global_device_ids=true, to_apply=%region_6.7 | all-reduce | flops 512 | bytes 4096 | tf_op jit(solution)/shard_map/psum | solution.py:177
  55.9 22.3 %all-gather = f32[16,1,256]{2,1,0:T(1,128)S(1)} all-gather(f32[1,1,256]{2,1,0:T(1,128)S(1)} %bitcast.177), channel_id=1, replica_groups=mesh['row'=16,'col'=2] {'row'}, dimensions={0}, use_global_device_ids=true | all-gather | bytes 17408 | tf_op jit(solution)/shard_map/all_gather | solution.py:180
  78.4 3.1 %while.38 = (s32[]{:T(128)}, f32[4,4,128]{2,0,1:T(4,128)S(1)}, s32[]{:T(128)}, s32[32]{0:T(128)S(1)}, f32[32]{0:T(128)S(1)}, /*index=5*/f32[32]{0:T(128)S(1)}, f...) while((s32[]{:T(128)}, f32[4,4,128]{2,0,1:T(4,128)S(1)}, ...), condition=%wide.region_11.14_spmd.clone, body=%wide.region_7.13_spmd.clone.sunk | while | flops 3619922 | bytes 1462743 | solution.py:135
  78.5 0.6 gather_fusion.3
  79.1 0.6 gather_fusion.2
  79.8 0.3 fusion.116
  80.2 0.5 fusion.120
  80.8 0.5 fusion.121
  81.5 12.4 %psum.15 = f32[512]{0:T(512)S(1)} all-reduce(f32[512]{0:T(512)S(1)} %slice_bitcast_fusion), channel_id=1, replica_groups=mesh['row'=16,'col'=2] {'col'}, use_global_device_ids=true, to_apply=%region_12.15 | all-reduce | flops 512 | bytes 4096 | tf_op jit(solution)/shard_map/psum | solution.py:184
  94.0 26.8 %all-gather.1 = f32[16,1,256]{2,1,0:T(1,128)S(1)} all-gather(f32[1,1,256]{2,1,0:T(1,128)S(1)} %bitcast.176), channel_id=1, replica_groups=mesh['row'=16,'col'=2] {'row'}, dimensions={0}, use_global_device_ids=true | all-gather | bytes 17408 | tf_op jit(solution)/shard_map/all_gather | solution.py:189
  120.9 3.2 %while.39 = (s32[]{:T(128)}, f32[4,3,128]{2,0,1:T(4,128)S(1)}, s32[]{:T(128)}, s32[32]{0:T(128)S(1)}, f32[32]{0:T(128)S(1)}, /*index=5*/f32[32]{0:T(128)S(1)}, f...) while((s32[]{:T(128)}, f32[4,3,128]{2,0,1:T(4,128)S(1)}, ...), condition=%wide.region_16.19_spmd.clone, body=%wide.region_13.18_spmd.clone.sunk | while | flops 4188242 | bytes 1489367 | solution.py:135
  121.0 0.6 gather_fusion.5
  121.7 0.6 gather_fusion.4
  122.8 0.6 fusion.127
  123.4 0.5 fusion.128
  124.1 0.9 copy.51
  125.0 29.8 %reduce-scatter.4.cloned.1.call-done = f32[256,3]{1,0:T(8,128)} async-done(((f32[512,3]{1,0:T(8,128)}), f32[256,3]{1,0:T(8,128)}) %reduce-scatter.4.cloned.1.call-update) | async-done | bytes 3088
  154.8 1.0 copy.50
  155.7 0.6 multiply_add_fusion
  (90 shorter events, 3.1 us)
Async XLA Ops:
  7.2 147.6 %reduce-scatter.4.cloned.1.call-start = ((), (), s32[]{:S(2)}) async-start(), calls=%async_computation.1 | async-start | bytes 393216
  9.3 0.7 copy-start.8
  9.9 0.7 copy-start.5
  10.6 0.7 copy-start.2
  10.6 0.7 copy-start.6
  10.7 0.7 copy-start.1
  11.4 0.7 copy-start.4
  11.4 0.7 copy-start.9
  12.1 5.3 %copy-start = (f32[10,256]{1,0:T(8,128)}, f32[10,256]{1,0:T(8,128)S(1)}, u32[]{:S(2)}) copy-start(f32[10,256]{1,0:T(8,128)S(1)} %pad_maximum_fusion.4) | copy-start | bytes 30724
  17.5 0.7 copy-start.7
  18.2 0.7 slice-start
  155.7 0.6 copy-start.3
Sparse Core Ops, SparseCore 0:
  125.1 29.6 reduce-scatter.3
where the time goes:
time: 164 us; the launch traced here: 163 us
  blocking collectives  101 us (62%)
  waiting for transfers between devices  29.8 us (18%)
  between operations  14.9 us (9%)
  local copies, waits for them, and re-layouts  9.93 us (6%)
  other arithmetic  6.46 us (4%)
    unnamed x2, waiting for transfers between devices  29.8 us
    all_gather x1, blocking collectives, body(): chain_j = lax.all_gather(chain_own, 'row', axis=0, tiled=True)  26.8 us
    all_gather x1, blocking collectives, body(): side_j = lax.all_gather(own_data[0:7], 'row', axis=1, tiled=True)  22.5 us
    all_gather x1, blocking collectives, body(): radius_j = lax.all_gather(radius_own, 'row', axis=0, tiled=True)  22.3 us
    psum x1, blocking collectives, body(): grad_all = lax.psum(pair_part[3], 'col')  12.4 us
    psum x1, blocking collectives, body(): born_all = lax.psum(born_part, 'col')  11.9 us
    all_gather x1, blocking collectives, body(): side_i = lax.all_gather(own_data, 'col', axis=1, tiled=True)  5.34 us
    unnamed x25, local copies, waits for them, and re-layouts  5.24 us
  transfers between devices with their start and end apart: 1, of which 1 were waited for; matrix products, arithmetic and copies ran while one was open for 0% of the time, Pallas kernels for 0%

commit v1 on v0

--- a/solution.py
+++ b/solution.py
@@ -153,7 +153,7 @@
     )
     own_data = jnp.concatenate([new_positions, charges[None, :], params[0:6]], axis=0)
     side_i = lax.all_gather(own_data, "col", axis=1, tiled=True)
-    side_j = lax.all_gather(own_data[0:7], "row", axis=1, tiled=True)
+    side_j = jnp.concatenate(lax.all_gather(own_data[0:7], "row"), axis=1)
     blocks_i = col_count * BLK_DEV
     blocks_j = row_count * BLK_DEV
     pack_i = side_i.reshape(10, blocks_i, TILE)

time: 164 us -> 163 us (level)
    unnamed x25 -> x24, local copies, waits for them, and re-layouts: 5.24 us -> 5.23 us
where the time goes in v1:
time: 163 us
  blocking collectives  101 us (62%)
  waiting for transfers between devices  29.8 us (18%)
  between operations  14.9 us (9%)
  local copies, waits for them, and re-layouts  9.24 us (6%)
  other arithmetic  6.46 us (4%)
    unnamed x2, waiting for transfers between devices  29.8 us
    all_gather x1, blocking collectives, body(): chain_j = lax.all_gather(chain_own, 'row', axis=0, tiled=True)  26.8 us
    all_gather x1, blocking collectives, body(): side_j = jnp.concatenate(lax.all_gather(own_data[0:7], 'row'), axis=1)  22.5 us
    all_gather x1, blocking collectives, body(): radius_j = lax.all_gather(radius_own, 'row', axis=0, tiled=True)  22.3 us
    psum x1, blocking collectives, body(): grad_all = lax.psum(pair_part[3], 'col')  12.4 us
    psum x1, blocking collectives, body(): born_all = lax.psum(born_part, 'col')  11.9 us
    all_gather x1, blocking collectives, body(): side_i = lax.all_gather(own_data, 'col', axis=1, tiled=True)  5.34 us
    unnamed x24, local copies, waits for them, and re-layouts  5.23 us
  transfers between devices with their start and end apart: 1, of which 1 were waited for; matrix products, arithmetic and copies ran while one was open for 0% of the time, Pallas kernels for 0%

profile of v1, /device:TPU:0, one launch (start us, length us, event | category | flops | bytes accessed | tf_op | source)
XLA Modules:
  0.0 162.5 jit_solution(17185935407784882806)
XLA Ops:
  7.2 1.4 maximum_bitcast_fusion
  9.3 0.7 copy-done.7
  9.9 0.7 copy-done.4
  10.8 0.6 copy-done.1
  11.4 0.7 copy-done.8
  12.1 5.3 %all_gather.15 = f32[10,512]{1,0:T(8,128)S(1)} all-gather(f32[10,256]{1,0:T(8,128)S(1)} %pad_maximum_fusion.4), channel_id=1, replica_groups=mesh['row'=16,'col'=2] {'col'}, dimensions={1}, use_global_device_ids=true | all-gather | bytes 30720 | tf_op jit(solution)/shard_map/all_gather | solution.py:155
  17.5 0.7 copy-done.6
  18.2 22.5 %all-gather.1 = f32[16,7,256]{2,1,0:T(8,128)S(1)} all-gather(f32[1,7,256]{2,1,0:T(8,128)S(1)} %slice_bitcast_fusion), channel_id=2, replica_groups=mesh['row'=16,'col'=2] {'row'}, dimensions={0}, use_global_device_ids=true | all-gather | bytes 121856 | tf_op jit(solution)/shard_map/all_gather | solution.py:156
  40.8 2.5 %while.37 = (s32[]{:T(128)}, f32[4,1,128]{2,0,1:T(4,128)S(1)}, s32[]{:T(128)}, s32[32]{0:T(128)S(1)}, f32[32]{0:T(128)S(1)}, /*index=5*/f32[32]{0:T(128)S(1)}, f...) while((s32[]{:T(128)}, f32[4,1,128]{2,0,1:T(4,128)S(1)}, ...), condition=%wide.region_5.6_spmd.clone, body=%wide.region_2.5_spmd.clone.sunk | while | flops 2036306 | bytes 881111 | solution.py:135
  40.9 0.6 gather_fusion.1
  41.6 0.6 gather_fusion
  42.2 0.3 multiply_reduce_fusion.3
  42.7 0.4 fusion.112
  43.3 11.9 %psum.14 = f32[512]{0:T(512)S(1)} all-reduce(f32[512]{0:T(512)S(1)} %bitcast.175), channel_id=1, replica_groups=mesh['row'=16,'col'=2] {'col'}, use_global_device_ids=true, to_apply=%region_6.7 | all-reduce | flops 512 | bytes 4096 | tf_op jit(solution)/shard_map/psum | solution.py:177
  55.3 22.3 %all-gather.2 = f32[16,1,256]{2,1,0:T(1,128)S(1)} all-gather(f32[1,1,256]{2,1,0:T(1,128)S(1)} %bitcast.179), channel_id=1, replica_groups=mesh['row'=16,'col'=2] {'row'}, dimensions={0}, use_global_device_ids=true | all-gather | bytes 17408 | tf_op jit(solution)/shard_map/all_gather | solution.py:180
  77.7 3.1 %while.38 = (s32[]{:T(128)}, f32[4,4,128]{2,0,1:T(4,128)S(1)}, s32[]{:T(128)}, s32[32]{0:T(128)S(1)}, f32[32]{0:T(128)S(1)}, /*index=5*/f32[32]{0:T(128)S(1)}, f...) while((s32[]{:T(128)}, f32[4,4,128]{2,0,1:T(4,128)S(1)}, ...), condition=%wide.region_11.14_spmd.clone, body=%wide.region_7.13_spmd.clone.sunk | while | flops 3619922 | bytes 1462743 | solution.py:135
  77.8 0.6 gather_fusion.3
  78.5 0.6 gather_fusion.2
  79.1 0.3 fusion.116
  79.6 0.5 fusion.120
  80.1 0.5 fusion.121
  80.8 12.4 %psum.15 = f32[512]{0:T(512)S(1)} all-reduce(f32[512]{0:T(512)S(1)} %slice_bitcast_fusion.1), channel_id=1, replica_groups=mesh['row'=16,'col'=2] {'col'}, use_global_device_ids=true, to_apply=%region_12.15 | all-reduce | flops 512 | bytes 4096 | tf_op jit(solution)/shard_map/psum | solution.py:184
  93.3 26.8 %all-gather.3 = f32[16,1,256]{2,1,0:T(1,128)S(1)} all-gather(f32[1,1,256]{2,1,0:T(1,128)S(1)} %bitcast.178), channel_id=1, replica_groups=mesh['row'=16,'col'=2] {'row'}, dimensions={0}, use_global_device_ids=true | all-gather | bytes 17408 | tf_op jit(solution)/shard_map/all_gather | solution.py:189
  120.2 3.2 %while.39 = (s32[]{:T(128)}, f32[4,3,128]{2,0,1:T(4,128)S(1)}, s32[]{:T(128)}, s32[32]{0:T(128)S(1)}, f32[32]{0:T(128)S(1)}, /*index=5*/f32[32]{0:T(128)S(1)}, f...) while((s32[]{:T(128)}, f32[4,3,128]{2,0,1:T(4,128)S(1)}, ...), condition=%wide.region_16.19_spmd.clone, body=%wide.region_13.18_spmd.clone.sunk | while | flops 4188242 | bytes 1489367 | solution.py:135
  120.3 0.6 gather_fusion.5
  121.0 0.6 gather_fusion.4
  122.1 0.6 fusion.127
  122.7 0.5 fusion.128
  123.4 0.9 copy.45
  124.3 29.8 %reduce-scatter.4.cloned.1.call-done = f32[256,3]{1,0:T(8,128)} async-done(((f32[512,3]{1,0:T(8,128)}), f32[256,3]{1,0:T(8,128)}) %reduce-scatter.4.cloned.1.call-update) | async-done | bytes 3088
  154.1 1.0 copy.44
  155.1 0.6 multiply_add_fusion
  (87 shorter events, 2.8 us)
Async XLA Ops:
  7.2 146.9 %reduce-scatter.4.cloned.1.call-start = ((), (), s32[]{:S(2)}) async-start(), calls=%async_computation.1 | async-start | bytes 393216
  9.3 0.7 copy-start.7
  9.9 0.7 copy-start.4
  10.6 0.7 copy-start.1
  10.6 0.7 copy-start.5
  10.7 0.7 copy-start
  11.4 0.7 copy-start.3
  11.4 0.7 copy-start.8
  17.5 0.7 copy-start.6
  155.1 0.6 copy-start.2
Sparse Core Ops, SparseCore 0:
  124.4 29.6 reduce-scatter.3
